TPU v7x, 8 devices: a whole 2x2x1 slice. The times are simulated.
8 devices in a mesh: sys: 1 (over z), aux: 2 (over y), orb: 4 (over x, core).
Axes of the slice: x: 2, y: 2, z: 1, core: 2. Of those that a mesh axis runs over, the one named last changes fastest.
Arguments:
- fit_tensor: float32 [1020, 348, 348], P(('sys', 'aux'), 'orb')
- occ_orbitals: float32 [348, 30], P('sys')
Outputs:
- output: float32 [348, 348], P(('sys', 'orb'), 'aux')
All inputs are finite; a program needn't handle non-finite values.
Results may differ from a plain program's by a relative error of at most 0.001.
Values are sent between devices in bfloat16 or wider.
A program may use at most 1 GiB of HBM per device.

v0:
```python
import jax
import jax.numpy as jnp
from jax import lax
from jax.sharding import PartitionSpec as P

PREC_MODE = lax.Precision.HIGHEST


def solution(mesh):
    n_orb = mesh.shape['orb']
    half_steps = n_orb // 2
    shift_perm = [(src, (src - 1) % n_orb) for src in range(n_orb)]

    def local_fock(fit_loc, orbitals):
        q_loc, row_blk, n_bf = fit_loc.shape
        n_occ = orbitals.shape[1]
        my_orb = lax.axis_index('orb')
        own_rows = lax.dynamic_slice_in_dim(orbitals, my_orb * row_blk, row_blk, 0)
        dens_rows = jnp.einsum('mi,si->ms', own_rows, orbitals, precision=PREC_MODE, preferred_element_type=jnp.float32)
        fit_flat = fit_loc.reshape(q_loc, row_blk * n_bf)
        coef_part = jnp.dot(fit_flat, dens_rows.reshape(row_blk * n_bf), precision=PREC_MODE, preferred_element_type=jnp.float32)
        aux_coef = lax.psum(coef_part, 'orb')
        coul_rows = jnp.dot(aux_coef, fit_flat, precision=PREC_MODE, preferred_element_type=jnp.float32).reshape(row_blk, n_bf)
        half_t = jnp.dot(fit_loc.reshape(q_loc * row_blk, n_bf), orbitals, precision=PREC_MODE, preferred_element_type=jnp.float32).reshape(q_loc, row_blk, n_occ)

        def exch_block(t_other):
            return jnp.einsum('qmi,qni->mn', half_t, t_other, precision=PREC_MODE, preferred_element_type=jnp.float32)

        blocks = jnp.zeros((row_blk, n_orb, row_blk), jnp.float32)
        blocks = lax.dynamic_update_slice(blocks, exch_block(half_t)[:, None, :], (0, my_orb, 0))

        def pass_step(pass_idx, loop_state):
            t_moving, acc_blocks = loop_state
            t_moving = lax.ppermute(t_moving, 'orb', shift_perm)
            col_blk = (my_orb + pass_idx) % n_orb
            acc_blocks = lax.dynamic_update_slice(acc_blocks, exch_block(t_moving)[:, None, :], (0, col_blk, 0))
            return t_moving, acc_blocks

        blocks = lax.fori_loop(1, half_steps + 1, pass_step, (half_t, blocks))[1]
        mirror_out = jnp.transpose(blocks, (1, 2, 0))
        mirror_in = lax.all_to_all(mirror_out, 'orb', 0, 0, tiled=True)
        mirror_rows = jnp.transpose(mirror_in, (1, 0, 2))
        col_dist = (jnp.arange(n_orb) - my_orb) % n_orb
        keep_own = (col_dist <= half_steps)[None, :, None]
        exch_rows = jnp.where(keep_own, blocks, mirror_rows).reshape(row_blk, n_bf)
        g_part = 2.0 * coul_rows - exch_rows
        return lax.psum_scatter(g_part, 'aux', scatter_dimension=1, tiled=True)

    spec_fit = P(('sys', 'aux'), 'orb', None)
    spec_orbitals = P('sys', None)
    spec_out = P(('sys', 'orb'), 'aux')
    return jax.shard_map(local_fock, mesh=mesh, in_specs=(spec_fit, spec_orbitals), out_specs=spec_out, check_vma=False)
```

profile of v0, /device:TPU:0, one launch (start us, length us, event | category | flops | bytes accessed | tf_op | source)
XLA Modules:
  0.0 459.1 jit_solution(17875529044640416835)
XLA Ops:
  6.5 0.8 copy-done
  7.3 43.1 %fusion.5 = f32[510,87,30]{0,2,1:T(8,128)S(1)} fusion(f32[510,87,348]{0,2,1:T(8,128)} %param.4, f32[348,30]{0,1:T(8,128)S(1)} %copy-done), kind=kOutput, calls=%fused_computation.10 | convolution fusion | flops 5558673408 | bytes 67129200 | tf_op jit(solution)/shard_map/dot_general | solution.py:24
  50.4 3.1 copy.11
  53.5 2.3 copy-done.2
  55.9 2.3 copy.25
  58.2 8.7 %fusion.1 = f32[87,4,87]{2,0,1:T(8,128)S(1)} fusion(f32[87,4,87]{2,0,1:T(8,128)S(1)} %broadcast_in_dim.26, s32[]{:T(128)S(6)} %select_n.52, f32[510,87,30]{0,1,2:T(8,128)} %copy-done.2), kind=kOutput, calls=%fused_computation.4 | convolution fusion | flops 1389668352 | bytes 10858500 | tf_op jit(solution)/shard_map/qmi,qni->mn/dot_general | solution.py:27
  66.9 147.0 %while.17 = (s32[]{:T(128)}, f32[510,87,30]{0,1,2:T(8,128)}, f32[87,4,87]{2,0,1:T(8,128)S(1)}, f32[510,87,30]{0,1,2:T(8,128)}, s32[]{:T(128)}, /*index=5*/s32[]{:T(128)}, s32[]{:T(128)}, s32[]{:T(128)}, s32[]{:T(128)}) while((s32[]{:T(128)}, f32[510,87,30]{0,1,2:T(8,128)}, f32[87,4,87]{2,0,1:T(8,128)S(1)}, f32[510,87,30]{0,1,2:T(8,128)}, ...), condition=%wide.region_2.3_spmd, body=%wide.region_1.2_spmd.sunk | while | flops 1389668352 | bytes 58943068 | solution.py:39
  66.9 2.8 collective-permute-start
  69.8 59.0 %collective-permute-done = f32[510,87,30]{0,1,2:T(8,128)} collective-permute-done((f32[510,87,30]{0,1,2:T(8,128)}, f32[510,87,30]{0,1,2:T(8,128)}, u32[]{:S(2)}, u32[]{:S(2)}) %collective-permute-start) | collective-permute-done | bytes 5324432 | tf_op jit(solution)/shard_map/while/body/eval_jaxpr/ppermute | solution.py:34
  128.7 5.5 %copy.31 = f32[510,87,30]{0,1,2:T(8,128)} copy(f32[510,87,30]{0,1,2:T(8,128)} %collective-permute-done) | data formatting | bytes 10648800 | tf_op jit(solution)/shard_map/while
  134.3 6.6 %fusion.26 = f32[87,4,87]{2,0,1:T(8,128)S(1)} fusion(f32[87,4,87]{2,0,1:T(8,128)S(1)} %get-tuple-element.201, s32[]{:T(128)S(6)} %select_n.61, f32[510,87,30]{0,1,2:T(8,128)S(1)} %bitcast.46, f32[510,87,30]{0,1,2:T(8,128)} %collective-permute-done), kind=kOutput, calls=%fused_computation.1.clone.1 | convolution fusion | flops 1389668352 | bytes 10776180 | tf_op jit(solution)/shard_map/while/body/eval_jaxpr/qmi,qni->mn/dot_general | solution.py:27
  140.9 1.9 collective-permute-start
  142.8 59.0 %collective-permute-done = f32[510,87,30]{0,1,2:T(8,128)} collective-permute-done((f32[510,87,30]{0,1,2:T(8,128)}, f32[510,87,30]{0,1,2:T(8,128)}, u32[]{:S(2)}, u32[]{:S(2)}) %collective-permute-start) | collective-permute-done | bytes 5324432 | tf_op jit(solution)/shard_map/while/body/eval_jaxpr/ppermute | solution.py:34
  201.8 5.5 %copy.31 = f32[510,87,30]{0,1,2:T(8,128)} copy(f32[510,87,30]{0,1,2:T(8,128)} %collective-permute-done) | data formatting | bytes 10648800 | tf_op jit(solution)/shard_map/while
  207.3 6.6 %fusion.26 = f32[87,4,87]{2,0,1:T(8,128)S(1)} fusion(f32[87,4,87]{2,0,1:T(8,128)S(1)} %get-tuple-element.201, s32[]{:T(128)S(6)} %select_n.61, f32[510,87,30]{0,1,2:T(8,128)S(1)} %bitcast.46, f32[510,87,30]{0,1,2:T(8,128)} %collective-permute-done), kind=kOutput, calls=%fused_computation.1.clone.1 | convolution fusion | flops 1389668352 | bytes 10776180 | tf_op jit(solution)/shard_map/while/body/eval_jaxpr/qmi,qni->mn/dot_general | solution.py:27
  213.9 0.8 copy.13
  214.7 3.4 all-to-all-start
  218.1 0.0 all-reduce.3.cloned.1.call-start
  218.1 57.9 %reshape.29 = f32[510,30276]{0,1:T(8,128)} reshape(f32[510,87,348]{0,2,1:T(8,128)} %param.4) | data formatting | bytes 123526080 | tf_op jit(solution)/shard_map/reshape | solution.py:20
  276.0 0.4 convolution_bitcast_fusion.1
  276.5 34.3 %fusion.3 = f32[1,510,1]{1,0,2:T(1,128)S(1)} fusion(f32[510,87,348]{0,2,1:T(8,128)} %param.4, f32[87,348,1]{1,0,2:T(8,128)S(1)} %convolution_bitcast_fusion.1), kind=kOutput, calls=%fused_computation.8 | convolution fusion | flops 185289120 | bytes 61886184 | tf_op jit(solution)/shard_map/dot_general | solution.py:21
  310.7 7.6 %psum.7 = f32[510]{0:T(512)S(1)} all-reduce(f32[510]{0:T(512)S(1)} %bitcast.49), channel_id=1, replica_groups=mesh['sys'=1,'aux'=2,'orb'=4] {'orb'}, use_global_device_ids=true, to_apply=%region_0.0 | all-reduce | flops 510 | bytes 4080 | tf_op jit(solution)/shard_map/psum | solution.py:22
  318.3 57.8 %dot_general.32 = f32[87,348,510]{2,1,0:T(8,128)} reshape(f32[30276,510]{1,0:T(8,128)} %bitcast.47) | data formatting | bytes 123526080 | tf_op jit(solution)/shard_map/dot_general | solution.py:23
  376.1 57.5 %fusion.11 = f32[1,87,348]{2,0,1:T(1,128)S(1)} fusion(f32[510,1,1]{0,1,2:T(1,128)S(1)} %bitcast.48, f32[87,348,510]{2,1,0:T(8,128)} %dot_general.32), kind=kOutput, calls=%fused_computation.20 | convolution fusion | flops 185289120 | bytes 61886184 | tf_op jit(solution)/shard_map/dot_general | solution.py:23
  433.6 0.0 all-to-all-done
  433.6 0.1 bitcast_select_fusion
  433.7 0.1 reshape.30
  433.9 0.7 fusion.2
  434.6 0.0 all-reduce.3.cloned.1.call-update
  434.6 0.6 dynamic-slice
  435.8 14.8 %all-reduce.3.cloned.1.call-done = f32[87,348]{1,0:T(8,128)} async-done(((f32[87,348]{1,0:T(8,128)}), f32[87,348]{1,0:T(8,128)}) %all-reduce.3.cloned.1.call-update) | async-done | bytes 121120
  450.6 1.6 constant_dynamic-slice_fusion
  (19 shorter events, 0.1 us)
Async XLA Ops:
  6.5 0.8 copy-start
  53.5 2.4 copy-start.2
  66.9 61.8 %collective-permute-start = (f32[510,87,30]{0,1,2:T(8,128)}, f32[510,87,30]{0,1,2:T(8,128)}, u32[]{:S(2)}, u32[]{:S(2)}) collective-permute-start(f32[510,87,30]{0,1,2:T(8,128)} %get-tuple-element.200), channel_id=1, source_target_pairs={{0,3},{1,0},{2,1},{3,2},{4,7},{5,4},{6,5},{7,6}} | collective-permute-start | bytes 15973208 | tf_op jit(solution)/shard_map/while/body/eval_jaxpr/ppermute | solution.py:34
  69.8 64.5 %slice-start = ((s8[5406720]{0:T(1024)(128)(4,1)}), s8[1212416]{0:T(1024)(128)(4,1)S(1)}, s32[]{:S(2)}) async-start(s8[5406720]{0:T(1024)(128)(4,1)} %bitcast.45), calls=%async_computation.2 | async-start | bytes 2424832 | tf_op jit(solution)/shard_map/while
  69.8 64.5 %slice-start.1 = ((s8[5406720]{0:T(1024)(128)(4,1)}), s8[4194304]{0:T(1024)(128)(4,1)S(1)}, s32[]{:S(2)}) async-start(s8[5406720]{0:T(1024)(128)(4,1)} %bitcast.45), calls=%async_computation.3 | async-start | bytes 8388608 | tf_op jit(solution)/shard_map/while
  140.9 60.9 %collective-permute-start = (f32[510,87,30]{0,1,2:T(8,128)}, f32[510,87,30]{0,1,2:T(8,128)}, u32[]{:S(2)}, u32[]{:S(2)}) collective-permute-start(f32[510,87,30]{0,1,2:T(8,128)} %get-tuple-element.200), channel_id=1, source_target_pairs={{0,3},{1,0},{2,1},{3,2},{4,7},{5,4},{6,5},{7,6}} | collective-permute-start | bytes 15973208 | tf_op jit(solution)/shard_map/while/body/eval_jaxpr/ppermute | solution.py:34
  142.8 64.5 %slice-start = ((s8[5406720]{0:T(1024)(128)(4,1)}), s8[1212416]{0:T(1024)(128)(4,1)S(1)}, s32[]{:S(2)}) async-start(s8[5406720]{0:T(1024)(128)(4,1)} %bitcast.45), calls=%async_computation.2 | async-start | bytes 2424832 | tf_op jit(solution)/shard_map/while
  142.8 64.5 %slice-start.1 = ((s8[5406720]{0:T(1024)(128)(4,1)}), s8[4194304]{0:T(1024)(128)(4,1)S(1)}, s32[]{:S(2)}) async-start(s8[5406720]{0:T(1024)(128)(4,1)} %bitcast.45), calls=%async_computation.3 | async-start | bytes 8388608 | tf_op jit(solution)/shard_map/while
  214.7 218.9 %all-to-all-start = ((f32[4,87,87]{2,1,0:T(8,128)}), f32[4,87,87]{2,1,0:T(8,128)S(1)}, u32[]{:S(2)}, u32[]{:S(2)}) async-start(f32[4,87,87]{2,1,0:T(8,128)} %bitcast.10), calls=%async_computation | async-start | bytes 360448 | tf_op jit(solution)/shard_map/all_to_all | solution.py:41
  218.1 232.5 %all-reduce.3.cloned.1.call-start = ((), (), s32[]{:S(2)}) async-start(), calls=%async_computation.1 | async-start | bytes 270336
  376.1 58.5 %copy-start.3 = (u32[8]{0:T(128)S(1)}, u32[8]{0:T(128)}, u32[]{:S(2)}) copy-start(u32[8]{0:T(128)} %constant.81) | copy-start | bytes 100
  376.1 76.2 %copy-start.1 = (f32[348,30]{0,1:T(8,128)S(1)}, f32[348,30]{0,1:T(8,128)}, u32[]{:S(2)}) copy-start(f32[348,30]{0,1:T(8,128)} %param.5) | copy-start | bytes 125284
Sparse Core Ops, SparseCore 0:
  434.7 15.8 all-reduce.2
where the time goes:
time: 462 us; the launch traced here: 459 us
  matrix products  157 us (34%)
  local copies, waits for them, and re-layouts  139 us (30%)
  waiting for transfers between devices  133 us (29%)
  between operations  14.2 us (3%)
  starting transfers between devices  8.15 us (2%)
  blocking collectives  7.55 us (2%)
    ppermute x2, waiting for transfers between devices, pass_step(): t_moving = lax.ppermute(t_moving, 'orb', shift_perm)  118 us
    reshape x1, local copies, waits for them, and re-layouts, local_fock(): fit_flat = fit_loc.reshape(q_loc, row_blk * n_bf)  57.9 us
    dot_general x1, local copies, waits for them, and re-layouts, local_fock(): jnp.dot(aux_coef, fit_flat, precision=PREC_MODE, preferred_element_type=j...  57.8 us
    dot_general x1, matrix products, local_fock(): jnp.dot(aux_coef, fit_flat, precision=PREC_MODE, preferred_element_type=j...  57.5 us
    dot_general x1, matrix products, local_fock(): jnp.dot(fit_loc.reshape(q_loc * row_blk, n_bf), orbitals, precision=PREC_...  43.1 us
    dot_general x1, matrix products, local_fock(): jnp.dot(fit_flat, dens_rows.reshape(row_blk * n_bf), precision=PREC_MODE,...  34.3 us
    dot_general x3, matrix products, exch_block(): jnp.einsum('qmi,qni->mn', half_t, t_other, precision=PREC_MODE, preferred...  21.8 us
    unnamed x2, waiting for transfers between devices  14.8 us
  transfers between devices with their start and end apart: 4, of which 3 were waited for; matrix products, arithmetic and copies ran while one was open for 45% of the time, Pallas kernels for 0%

commit v1 on v0

v1 whole, which is shorter than its diff:
```python
import jax
import jax.numpy as jnp
from jax import lax
from jax.experimental import pallas as pl
from jax.experimental.pallas import tpu as pltpu
from jax.sharding import PartitionSpec as P

f32 = jnp.float32
bf16 = jnp.bfloat16

NOCC = 30
ROWS = 87
RPAD = 88
NBF = 348
NQ = 510
QT = 4
GRP = 8
NGRP = 11
RING = 3
EARLY = 4
ICH = 3
NCH = NOCC // ICH
HALF = 174


def pieces(x):
    hi = x.astype(bf16)
    rest = x - hi.astype(f32)
    mid = rest.astype(bf16)
    low = (rest - mid.astype(f32)).astype(bf16)
    return hi, mid, low


def pieces32(x):
    hi = x.astype(bf16).astype(f32)
    rest = x - hi
    mid = rest.astype(bf16).astype(f32)
    return hi, mid, rest - mid


def dot_nt(a, b):
    return lax.dot_general(a, b, (((1,), (1,)), ((), ())), preferred_element_type=f32)


def full_nt(a, b):
    n = a.shape[0]
    ah, am, al = pieces32(a)
    bh, bm, bl = pieces32(b)
    first = dot_nt(jnp.concatenate([ah, am, al], axis=0), bh)
    second = dot_nt(jnp.concatenate([ah, am], axis=0), bm)
    third = dot_nt(ah, bl)
    small = (first[2 * n:] + second[n:]) + third
    return first[:n] + ((first[n:2 * n] + second[:n]) + small)


def kernel(bt, ct, out, ring, tb, sb, rb, gacc, cst, cown, gown, grecv, jt, ks, kr, rsend, rrecv,
           pf, ph, dma_sem, d2d_s, d2d_r, ici_s, ici_r, g_s, g_r, r_s, r_r, p_s, p_r):
    y = lax.axis_index('aux')
    o = lax.axis_index('orb')
    p = o // 2
    s = lax.rem(o, 2)
    sib = o + 1 - 2 * s
    opp = lax.rem(o + 2, 4)
    opp_sib = 3 - o
    yo = 1 - y
    keep = 2 * p
    give = 2 * (1 - p)

    def dev(yy, oo):
        return {'aux': yy, 'orb': oo}

    def remote(src, dst, ssem, rsem, to):
        return pltpu.make_async_remote_copy(src_ref=src, dst_ref=dst, send_sem=ssem, recv_sem=rsem,
                                            device_id=to, device_id_type=pl.DeviceIdType.MESH)

    def load(step, j):
        m = lax.rem(step, NGRP) * GRP + j
        slot = lax.rem(step, RING) * GRP + j
        return m, pltpu.make_async_copy(bt.at[m], ring.at[slot], dma_sem.at[slot])

    def start_group(step):
        for j in range(GRP):
            m, copy = load(step, j)

            @pl.when(m < ROWS)
            def _():
                copy.start()

    def wait_group(step):
        for j in range(GRP):
            m, copy = load(step, j)

            @pl.when(m < ROWS)
            def _():
                copy.wait()

    for step in range(RING - 1):
        start_group(step)

    barrier = pltpu.get_barrier_semaphore()
    peers = [(y, sib), (y, opp), (y, opp_sib), (yo, o), (yo, sib), (yo, opp), (yo, opp_sib)]
    for peer in peers:
        pl.semaphore_signal(barrier, inc=1, device_id=dev(*peer), device_id_type=pl.DeviceIdType.MESH)
    pl.semaphore_wait(barrier, len(peers))

    t4 = tb.reshape(QT, NOCC, RPAD, 128)

    def early_copy(g):
        rows = pl.ds(pl.multiple_of(g * GRP, GRP), GRP)
        return remote(t4.at[pl.ds(give, 2), :, rows], rb.at[:, :, rows], ici_s.at[g], ici_r.at[g], dev(y, opp))

    def late_copy(c):
        orbs = pl.ds(c * ICH, ICH)
        rows = pl.ds(EARLY * GRP, RPAD - EARLY * GRP)
        return remote(t4.at[pl.ds(give, 2), orbs, rows], rb.at[:, orbs, rows],
                      ici_s.at[EARLY + c], ici_r.at[EARLY + c], dev(y, opp))

    def sib_copy(g):
        rows = pl.ds(pl.multiple_of(g * GRP, GRP), GRP)
        return remote(t4.at[:, :, rows], sb.at[:, :, rows], d2d_s.at[g], d2d_r.at[g], dev(y, sib))

    c = jnp.concatenate([ct[...], jnp.zeros((2, NBF), f32)], axis=0)
    cst[...] = jnp.concatenate(pieces(c), axis=0)
    mine = c[:, 0:ROWS]
    for b in range(1, 4):
        mine = jnp.where(o == b, c[:, b * ROWS:(b + 1) * ROWS], mine)
    cown[...] = jnp.concatenate([mine, jnp.zeros((32, 128 - ROWS), f32)], axis=1)
    gacc[...] = jnp.zeros_like(gacc)
    jt[...] = jnp.zeros_like(jt)
    ks[...] = jnp.zeros_like(ks)
    kr[...] = jnp.zeros_like(kr)

    def t_step(g, carry):
        start_group(g + RING - 1)
        wait_group(g)
        cg = pltpu.roll(cown[...], lax.rem(128 - g * GRP, 128), 1)
        for j in range(GRP):
            m = g * GRP + j
            x = ring[lax.rem(g, RING) * GRP + j]
            r = None
            for piece in pieces(x):
                term = jnp.dot(cst[...], piece, preferred_element_type=f32)
                r = term if r is None else r + term
            t = r[0:32] + r[32:64] + r[64:96]
            if j == GRP - 1:
                t = jnp.where(m < ROWS, t, 0.0)
            gacc[:, 0:NQ] += t * cg[:, j:j + 1]
            for k in range(QT):
                hi = min(NQ, 128 * (k + 1))
                tt = t[:NOCC, 128 * k:hi]
                if hi < 128 * (k + 1):
                    tt = jnp.concatenate([tt, jnp.zeros((NOCC, 128 * (k + 1) - hi), f32)], axis=1)
                tb[k, pl.ds(m, NOCC, stride=RPAD), :] = tt
        sib_copy(g).start()

        @pl.when(g < EARLY)
        def _():
            early_copy(g).start()
        return carry

    lax.fori_loop(0, NGRP, t_step, 0)

    gown[...] = jnp.sum(gacc[...], axis=0, keepdims=True)
    g_copies = [remote(gown, grecv.at[k], g_s.at[k], g_r.at[k], dev(y, to))
                for k, to in enumerate((sib, opp, opp_sib))]
    for copy in g_copies:
        copy.start()

    def late_start(c, carry):
        late_copy(c).start()
        return carry

    lax.fori_loop(0, NCH, late_start, 0)

    def sib_wait(g, carry):
        sib_copy(g).wait_recv()
        return carry

    lax.fori_loop(0, NGRP, sib_wait, 0)

    def both(tiles_own, tiles_sib):
        own = jnp.concatenate(tiles_own, axis=1)
        other = jnp.concatenate(tiles_sib, axis=1)
        gap = jnp.zeros((128 - RPAD, own.shape[1]), f32)
        return own, jnp.concatenate([own, gap, other], axis=0)

    def k_self(i):
        own, stack = both([t4[k, i] for k in range(QT)], [sb[k, i] for k in range(QT)])
        res = full_nt(own, stack)
        ks[:, 0:128 + RPAD] += res

    def self_step(i, carry):
        k_self(i)
        return carry

    ahead = NOCC - 2 * NGRP
    lax.fori_loop(0, ahead, self_step, 0)

    for copy in g_copies:
        copy.wait()
    gam = gown[...] + grecv[0] + grecv[1] + grecv[2]
    gown[...] = gam
    lane = lax.broadcasted_iota(jnp.int32, (NBF, 128), 1)

    def j_step(g, carry):
        step = g + NGRP

        @pl.when(step + RING - 1 < 2 * NGRP)
        def _():
            start_group(step + RING - 1)
        wait_group(step)
        gv = gown[:, 0:NQ]
        acc = jt[...]
        for j in range(GRP):
            x = ring[lax.rem(step, RING) * GRP + j]
            col = jnp.sum(x * gv, axis=1, keepdims=True)
            acc = jnp.where(lane == g * GRP + j, col, acc)
        jt[...] = acc
        k_self(ahead + 2 * g)
        k_self(ahead + 2 * g + 1)
        return carry

    lax.fori_loop(0, NGRP, j_step, 0)

    lane88 = lax.broadcasted_iota(jnp.int32, (RPAD, 128), 1)

    def columns(first, second):
        a = jnp.where(s == 0, first, second)
        b = pltpu.roll(jnp.where(s == 0, second, first), ROWS, 1)
        return jnp.concatenate([jnp.where(lane88 < ROWS, a, b), b], axis=1)[:, 0:HALF]

    jrows = jnp.transpose(jt[...])[0:RPAD]
    j0 = 2.0 * jrows[:, 0:HALF]
    j1 = 2.0 * jrows[:, HALF:2 * HALF]
    kself = columns(ks[:, 0:128], ks[:, 128:256])
    h0 = j0 - jnp.where(p == 0, kself, 0.0)
    h1 = j1 - jnp.where(p == 1, kself, 0.0)
    rsend[:, 0:HALF] = jnp.where(y == 0, h1, h0)
    base = jnp.where(y == 0, h0, h1)
    ks[:, 0:HALF] = base
    r_copy = remote(rsend, rrecv, r_s, r_r, dev(yo, o))
    r_copy.start()

    def early_wait(g, carry):
        early_copy(g).wait_recv()
        return carry

    lax.fori_loop(0, EARLY, early_wait, 0)

    def r_step(c, carry):
        late_copy(c).wait_recv()
        for di in range(ICH):
            i = c * ICH + di
            _, stack = both([t4[keep + k, i] for k in range(2)], [sb[keep + k, i] for k in range(2)])
            moved = jnp.concatenate([rb[k, i] for k in range(2)], axis=1)
            kr[:, 0:128 + RPAD] += full_nt(moved, stack)
        return carry

    lax.fori_loop(0, NCH, r_step, 0)

    p_full0 = remote(kr, pf.at[0], p_s.at[0], p_r.at[0], dev(y, opp))
    p_full1 = remote(kr, pf.at[1], p_s.at[0], p_r.at[1], dev(yo, opp))
    p_own = remote(kr.at[:, pl.ds(0, 128)], ph.at[0], p_s.at[1], p_r.at[2], dev(yo, o))
    p_sib0 = remote(kr.at[:, pl.ds(128, 128)], ph.at[1], p_s.at[2], p_r.at[3], dev(y, sib))
    p_sib1 = remote(kr.at[:, pl.ds(128, 128)], ph.at[2], p_s.at[2], p_r.at[4], dev(yo, sib))

    @pl.when(y == p)
    def _():
        for copy in (p_full0, p_sib1, p_own):
            copy.start()
        r_copy.wait()
        out[...] = (ks[:, 0:HALF] + rrecv[:, 0:HALF])[0:ROWS]
        for copy in (p_full0, p_sib1, p_own):
            copy.wait_send()

    @pl.when(y != p)
    def _():
        p_full1.start()
        p_sib0.start()
        r_copy.wait()
        for copy in (p_sib0, p_own, p_sib1):
            copy.wait_recv()
        col_opp = jnp.transpose(jnp.concatenate([kr[:, 0:128] + ph[0], jnp.zeros((40, 128), f32)], axis=0))[0:RPAD]
        col_sib = jnp.transpose(jnp.concatenate([ph[1] + ph[2], jnp.zeros((40, 128), f32)], axis=0))[0:RPAD]
        for copy in (p_full0, p_full1):
            copy.wait_recv()
        block_a = (pf[0, :, 0:128] + pf[1, :, 0:128]) + col_opp
        block_b = (pf[0, :, 128:256] + pf[1, :, 128:256]) + col_sib
        res = (ks[:, 0:HALF] + rrecv[:, 0:HALF]) - columns(block_a, block_b)
        out[...] = res[0:ROWS]
        p_full1.wait_send()
        p_sib0.wait_send()

    def sends_done(g, carry):
        sib_copy(g).wait_send()
        return carry

    lax.fori_loop(0, NGRP, sends_done, 0)

    def early_done(g, carry):
        early_copy(g).wait_send()
        return carry

    lax.fori_loop(0, EARLY, early_done, 0)

    def late_done(c, carry):
        late_copy(c).wait_send()
        return carry

    lax.fori_loop(0, NCH, late_done, 0)


def solution(mesh):
    sem = pltpu.SemaphoreType.DMA

    def local_fock(fit_loc, orbitals):
        bt = jnp.transpose(fit_loc, (1, 2, 0))
        ct = jnp.transpose(orbitals)
        return pl.pallas_call(
            kernel,
            out_shape=jax.ShapeDtypeStruct((ROWS, HALF), f32),
            in_specs=[pl.BlockSpec(memory_space=pl.ANY), pl.BlockSpec(memory_space=pltpu.VMEM)],
            out_specs=pl.BlockSpec(memory_space=pltpu.VMEM),
            scratch_shapes=[
                pltpu.VMEM((RING * GRP, NBF, NQ), f32),
                pltpu.VMEM((QT, NOCC * RPAD, 128), f32),
                pltpu.VMEM((QT, NOCC, RPAD, 128), f32),
                pltpu.VMEM((2, NOCC, RPAD, 128), f32),
                pltpu.VMEM((32, 512), f32),
                pltpu.VMEM((96, NBF), bf16),
                pltpu.VMEM((32, 128), f32),
                pltpu.VMEM((1, 512), f32),
                pltpu.VMEM((3, 1, 512), f32),
                pltpu.VMEM((NBF, 128), f32),
                pltpu.VMEM((RPAD, 256), f32),
                pltpu.VMEM((RPAD, 256), f32),
                pltpu.VMEM((RPAD, 256), f32),
                pltpu.VMEM((RPAD, 256), f32),
                pltpu.VMEM((2, RPAD, 256), f32),
                pltpu.VMEM((3, RPAD, 128), f32),
                sem((RING * GRP,)), sem((NGRP,)), sem((NGRP,)), sem((EARLY + NCH,)), sem((EARLY + NCH,)),
                sem((3,)), sem((3,)), sem, sem, sem((3,)), sem((5,)),
            ],
            compiler_params=pltpu.CompilerParams(collective_id=0, has_side_effects=True,
                                                 vmem_limit_bytes=60 << 20),
            name='fock',
        )(bt, ct)

    spec_fit = P(('sys', 'aux'), 'orb', None)
    spec_orbitals = P('sys', None)
    spec_out = P(('sys', 'orb'), 'aux')
    return jax.shard_map(local_fock, mesh=mesh, in_specs=(spec_fit, spec_orbitals), out_specs=spec_out, check_vma=False)
```

time: 462 us -> 76.2 us (0.16)
  matrix products: 157 us -> 0 us
  local copies, waits for them, and re-layouts: 139 us -> 1.53 us
  waiting for transfers between devices: 133 us -> 0 us
  Pallas kernels: 0 us -> 74.5 us
  between operations: 14.2 us -> 0.01 us
  starting transfers between devices: 8.15 us -> 0 us
  blocking collectives: 7.55 us -> 0 us
    dot_general x7 -> x0, matrix products: 157 us -> none  [the longest x1 57.5 us: local_fock(): jnp.dot(aux_coef, fit_flat, precision=PREC_MODE, preferred_element_type=j...]
    ppermute x2 -> x0, waiting for transfers between devices: 118 us -> none  [pass_step(): t_moving = lax.ppermute(t_moving, 'orb', shift_perm)]
    pallas_call x0 -> x1, Pallas kernels: none -> 74.5 us  [local_fock(): pl.pallas_call(kernel, out_shape=jax.ShapeDtypeStruct((ROWS, HALF), f32),...]
    reshape x2 -> x0, local copies, waits for them, and re-layouts: 58 us -> none  [the longest x1 57.9 us: local_fock(): fit_flat = fit_loc.reshape(q_loc, row_blk * n_bf)]
    dot_general x1 -> x0, local copies, waits for them, and re-layouts: 57.8 us -> none  [local_fock(): jnp.dot(aux_coef, fit_flat, precision=PREC_MODE, preferred_element_type=j...]
    while x12 -> x0, local copies, waits for them, and re-layouts: 15 us -> none
    unnamed x2 -> x0, waiting for transfers between devices: 14.8 us -> none
    psum x1 -> x0, blocking collectives: 7.55 us -> none  [local_fock(): aux_coef = lax.psum(coef_part, 'orb')]
  transfers between devices with their start and end apart: 4 -> 0, of which waited for: 3 -> 0; matrix products, arithmetic and copies ran while one was open for 45% -> 0% of each run, Pallas kernels for 0% -> 0%
where the time goes in v1:
time: 76.2 us; the launch traced here: 76 us
  Pallas kernels  74.5 us (98%)
  local copies, waits for them, and re-layouts  1.53 us (2%)
    pallas_call x1, Pallas kernels, local_fock(): pl.pallas_call(kernel, out_shape=jax.ShapeDtypeStruct((ROWS, HALF), f32),...  74.5 us
    unnamed x1, local copies, waits for them, and re-layouts  1.53 us

profile of v1, /device:TPU:0, one launch (start us, length us, event | category | flops | bytes accessed | tf_op | source)
XLA Modules:
  0.0 76.0 jit_solution(312403654728542945)
XLA Ops:
  0.0 74.5 %fock.1 = f32[87,174]{1,0:T(8,128)} custom-call(f32[87,348,510]{2,1,0:T(8,128)} %bitcast.2, f32[30,348]{1,0:T(8,128)} %bitcast.3), custom_call_target="tpu_custom_call" | custom-call | tf_op jit(solution)/shard_map/fock/pallas_call | solution.py:319
  74.5 1.5 %copy.4 = f32[87,174]{1,0:T(8,128)} copy(f32[87,174]{1,0:T(8,128)} %fock.1) | data formatting | bytes 121104

commit v2 on v1

--- a/solution.py
+++ b/solution.py
@@ -17,7 +17,8 @@
 GRP = 8
 NGRP = 11
 RING = 3
-EARLY = 4
+EARLY = 5
+FIRST = 2
 ICH = 3
 NCH = NOCC // ICH
 HALF = 174
@@ -53,8 +54,8 @@
     return first[:n] + ((first[n:2 * n] + second[:n]) + small)
 
 
-def kernel(bt, ct, out, ring, tb, sb, rb, gacc, cst, cown, gown, grecv, jt, ks, kr, rsend, rrecv,
-           pf, ph, dma_sem, d2d_s, d2d_r, ici_s, ici_r, g_s, g_r, r_s, r_r, p_s, p_r):
+def kernel(bt, ct_hbm, out, ring, ct, fb, e0, tb, sb, rb, gacc, cst, cown, gown, grecv, jt, ks, kr, rsend, rrecv,
+           pf, ph, dma_sem, ct_sem, fb_sem, e_s, e_r, d2d_s, d2d_r, ici_s, ici_r, g_s, g_r, r_s, r_r, p_s, p_r):
     y = lax.axis_index('aux')
     o = lax.axis_index('orb')
     p = o // 2
@@ -94,6 +95,14 @@
             def _():
                 copy.wait()
 
+    def first_load(m):
+        lanes = pl.ds(pl.multiple_of(give * 128, 128), 128)
+        return pltpu.make_async_copy(bt.at[m, :, lanes], fb.at[m], fb_sem.at[m])
+
+    ct_copy = pltpu.make_async_copy(ct_hbm, ct, ct_sem)
+    ct_copy.start()
+    for m in range(FIRST * GRP):
+        first_load(m).start()
     for step in range(RING - 1):
         start_group(step)
 
@@ -101,13 +110,23 @@
     peers = [(y, sib), (y, opp), (y, opp_sib), (yo, o), (yo, sib), (yo, opp), (yo, opp_sib)]
     for peer in peers:
         pl.semaphore_signal(barrier, inc=1, device_id=dev(*peer), device_id_type=pl.DeviceIdType.MESH)
-    pl.semaphore_wait(barrier, len(peers))
 
     t4 = tb.reshape(QT, NOCC, RPAD, 128)
 
     def early_copy(g):
         rows = pl.ds(pl.multiple_of(g * GRP, GRP), GRP)
         return remote(t4.at[pl.ds(give, 2), :, rows], rb.at[:, :, rows], ici_s.at[g], ici_r.at[g], dev(y, opp))
+
+    def early_rest(g):
+        rows = pl.ds(pl.multiple_of(g * GRP, GRP), GRP)
+        return remote(t4.at[pl.ds(give + 1, 1), :, rows], rb.at[pl.ds(1, 1), :, rows], ici_s.at[g], ici_r.at[g],
+                      dev(y, opp))
+
+    e4 = e0.reshape(FIRST, NOCC, GRP, 128)
+
+    def first_copy(g):
+        rows = pl.ds(g * GRP, GRP)
+        return remote(e4.at[g], rb.at[0, :, rows], e_s.at[g], e_r.at[g], dev(y, opp))
 
     def late_copy(c):
         orbs = pl.ds(c * ICH, ICH)
@@ -119,6 +138,7 @@
         rows = pl.ds(pl.multiple_of(g * GRP, GRP), GRP)
         return remote(t4.at[:, :, rows], sb.at[:, :, rows], d2d_s.at[g], d2d_r.at[g], dev(y, sib))
 
+    ct_copy.wait()
     c = jnp.concatenate([ct[...], jnp.zeros((2, NBF), f32)], axis=0)
     cst[...] = jnp.concatenate(pieces(c), axis=0)
     mine = c[:, 0:ROWS]
@@ -130,6 +150,22 @@
     ks[...] = jnp.zeros_like(ks)
     kr[...] = jnp.zeros_like(kr)
 
+    def t_rows(x):
+        r = None
+        for piece in pieces(x):
+            term = jnp.dot(cst[...], piece, preferred_element_type=f32)
+            r = term if r is None else r + term
+        return r[0:32] + r[32:64] + r[64:96]
+
+    for g in range(FIRST):
+        for j in range(GRP):
+            first_load(g * GRP + j).wait()
+        for j in range(GRP):
+            e0[pl.ds(g * NOCC * GRP + j, NOCC, stride=GRP), :] = t_rows(fb[g * GRP + j])[:NOCC]
+        if g == 0:
+            pl.semaphore_wait(barrier, len(peers))
+        first_copy(g).start()
+
     def t_step(g, carry):
         start_group(g + RING - 1)
         wait_group(g)
@@ -137,11 +173,7 @@
         for j in range(GRP):
             m = g * GRP + j
             x = ring[lax.rem(g, RING) * GRP + j]
-            r = None
-            for piece in pieces(x):
-                term = jnp.dot(cst[...], piece, preferred_element_type=f32)
-                r = term if r is None else r + term
-            t = r[0:32] + r[32:64] + r[64:96]
+            t = t_rows(x)
             if j == GRP - 1:
                 t = jnp.where(m < ROWS, t, 0.0)
             gacc[:, 0:NQ] += t * cg[:, j:j + 1]
@@ -153,7 +185,11 @@
                 tb[k, pl.ds(m, NOCC, stride=RPAD), :] = tt
         sib_copy(g).start()
 
-        @pl.when(g < EARLY)
+        @pl.when(g < FIRST)
+        def _():
+            early_rest(g).start()
+
+        @pl.when((g >= FIRST) & (g < EARLY))
         def _():
             early_copy(g).start()
         return carry
@@ -245,7 +281,10 @@
         early_copy(g).wait_recv()
         return carry
 
-    lax.fori_loop(0, EARLY, early_wait, 0)
+    for g in range(FIRST):
+        first_copy(g).wait_recv()
+        early_rest(g).wait_recv()
+    lax.fori_loop(FIRST, EARLY, early_wait, 0)
 
     def r_step(c, carry):
         late_copy(c).wait_recv()
@@ -301,7 +340,10 @@
         early_copy(g).wait_send()
         return carry
 
-    lax.fori_loop(0, EARLY, early_done, 0)
+    for g in range(FIRST):
+        first_copy(g).wait_send()
+        early_rest(g).wait_send()
+    lax.fori_loop(FIRST, EARLY, early_done, 0)
 
     def late_done(c, carry):
         late_copy(c).wait_send()
@@ -318,11 +360,14 @@
         ct = jnp.transpose(orbitals)
         return pl.pallas_call(
             kernel,
-            out_shape=jax.ShapeDtypeStruct((ROWS, HALF), f32),
-            in_specs=[pl.BlockSpec(memory_space=pl.ANY), pl.BlockSpec(memory_space=pltpu.VMEM)],
+            out_shape=pltpu.VMEM((ROWS, HALF), f32),
+            in_specs=[pl.BlockSpec(memory_space=pl.ANY), pl.BlockSpec(memory_space=pl.ANY)],
             out_specs=pl.BlockSpec(memory_space=pltpu.VMEM),
             scratch_shapes=[
                 pltpu.VMEM((RING * GRP, NBF, NQ), f32),
+                pltpu.VMEM((NOCC, NBF), f32),
+                pltpu.VMEM((FIRST * GRP, NBF, 128), f32),
+                pltpu.VMEM((FIRST * NOCC * GRP, 128), f32),
                 pltpu.VMEM((QT, NOCC * RPAD, 128), f32),
                 pltpu.VMEM((QT, NOCC, RPAD, 128), f32),
                 pltpu.VMEM((2, NOCC, RPAD, 128), f32),
@@ -338,7 +383,7 @@
                 pltpu.VMEM((RPAD, 256), f32),
                 pltpu.VMEM((2, RPAD, 256), f32),
                 pltpu.VMEM((3, RPAD, 128), f32),
-                sem((RING * GRP,)), sem((NGRP,)), sem((NGRP,)), sem((EARLY + NCH,)), sem((EARLY + NCH,)),
+                sem((RING * GRP,)), sem, sem((FIRST * GRP,)), sem((FIRST,)), sem((FIRST,)), sem((NGRP,)), sem((NGRP,)), sem((EARLY + NCH,)), sem((EARLY + NCH,)),
                 sem((3,)), sem((3,)), sem, sem, sem((3,)), sem((5,)),
             ],
             compiler_params=pltpu.CompilerParams(collective_id=0, has_side_effects=True,

time: 76.2 us -> 73.6 us (0.966)
  Pallas kernels: 74.5 us -> 72.8 us
  local copies, waits for them, and re-layouts: 1.53 us -> 0.64 us
    pallas_call x1, Pallas kernels: 74.5 us -> 72.8 us  [local_fock(): pl.pallas_call(kernel, out_shape=pltpu.VMEM((ROWS, HALF), f32), in_specs=...]
    unnamed x1, local copies, waits for them, and re-layouts: 1.53 us -> 0.64 us
where the time goes in v2:
time: 73.6 us; the launch traced here: 73.5 us
  Pallas kernels  72.8 us (99%)
    pallas_call x1, Pallas kernels, local_fock(): pl.pallas_call(kernel, out_shape=pltpu.VMEM((ROWS, HALF), f32), in_specs=...  72.8 us

profile of v2, /device:TPU:0, one launch (start us, length us, event | category | flops | bytes accessed | tf_op | source)
XLA Modules:
  0.0 73.5 jit_solution(10604550020898055986)
XLA Ops:
  0.0 72.8 %fock.1 = f32[87,174]{1,0:T(8,128)S(1)} custom-call(f32[87,348,510]{2,1,0:T(8,128)} %bitcast.2, f32[30,348]{1,0:T(8,128)} %bitcast.3), custom_call_target="tpu_custom_call" | custom-call | tf_op jit(solution)/shard_map/fock/pallas_call | solution.py:361
  72.9 0.6 copy.4

commit v3 on v2

--- a/solution.py
+++ b/solution.py
@@ -16,8 +16,10 @@
 QT = 4
 GRP = 8
 NGRP = 11
-RING = 3
-EARLY = 5
+RING = 7
+AHEAD = 2
+AGAIN = NGRP - RING
+EARLY = 6
 FIRST = 2
 ICH = 3
 NCH = NOCC // ICH
@@ -74,22 +76,22 @@
         return pltpu.make_async_remote_copy(src_ref=src, dst_ref=dst, send_sem=ssem, recv_sem=rsem,
                                             device_id=to, device_id_type=pl.DeviceIdType.MESH)
 
-    def load(step, j):
-        m = lax.rem(step, NGRP) * GRP + j
-        slot = lax.rem(step, RING) * GRP + j
+    def load(g, slot, j):
+        m = g * GRP + j
+        slot = slot * GRP + j
         return m, pltpu.make_async_copy(bt.at[m], ring.at[slot], dma_sem.at[slot])
 
-    def start_group(step):
-        for j in range(GRP):
-            m, copy = load(step, j)
+    def start_group(g, slot):
+        for j in range(GRP):
+            m, copy = load(g, slot, j)
 
             @pl.when(m < ROWS)
             def _():
-                copy.start()
-
-    def wait_group(step):
-        for j in range(GRP):
-            m, copy = load(step, j)
+                copy.start(priority=1)
+
+    def wait_group(g, slot):
+        for j in range(GRP):
+            m, copy = load(g, slot, j)
 
             @pl.when(m < ROWS)
             def _():
@@ -103,8 +105,8 @@
     ct_copy.start()
     for m in range(FIRST * GRP):
         first_load(m).start()
-    for step in range(RING - 1):
-        start_group(step)
+    for g in range(AHEAD):
+        start_group(g, g)
 
     barrier = pltpu.get_barrier_semaphore()
     peers = [(y, sib), (y, opp), (y, opp_sib), (yo, o), (yo, sib), (yo, opp), (yo, opp_sib)]
@@ -167,12 +169,16 @@
         first_copy(g).start()
 
     def t_step(g, carry):
-        start_group(g + RING - 1)
-        wait_group(g)
+        slot = lax.rem(g, RING)
+
+        @pl.when(g + AHEAD < NGRP)
+        def _():
+            start_group(g + AHEAD, lax.rem(g + AHEAD, RING))
+        wait_group(g, slot)
         cg = pltpu.roll(cown[...], lax.rem(128 - g * GRP, 128), 1)
         for j in range(GRP):
             m = g * GRP + j
-            x = ring[lax.rem(g, RING) * GRP + j]
+            x = ring[slot * GRP + j]
             t = t_rows(x)
             if j == GRP - 1:
                 t = jnp.where(m < ROWS, t, 0.0)
@@ -238,22 +244,26 @@
     gown[...] = gam
     lane = lax.broadcasted_iota(jnp.int32, (NBF, 128), 1)
 
-    def j_step(g, carry):
-        step = g + NGRP
-
-        @pl.when(step + RING - 1 < 2 * NGRP)
+    def j_step(n, carry):
+        g = lax.rem(n + AGAIN, NGRP)
+        slot = lax.rem(n + AGAIN, RING)
+
+        @pl.when((n >= 1) & (n <= AGAIN))
         def _():
-            start_group(step + RING - 1)
-        wait_group(step)
+            start_group(n - 1, lax.rem(n - 1 + AGAIN, RING))
+
+        @pl.when(n >= RING)
+        def _():
+            wait_group(g, slot)
         gv = gown[:, 0:NQ]
         acc = jt[...]
         for j in range(GRP):
-            x = ring[lax.rem(step, RING) * GRP + j]
+            x = ring[slot * GRP + j]
             col = jnp.sum(x * gv, axis=1, keepdims=True)
             acc = jnp.where(lane == g * GRP + j, col, acc)
         jt[...] = acc
-        k_self(ahead + 2 * g)
-        k_self(ahead + 2 * g + 1)
+        k_self(ahead + 2 * n)
+        k_self(ahead + 2 * n + 1)
         return carry
 
     lax.fori_loop(0, NGRP, j_step, 0)
@@ -387,7 +397,7 @@
                 sem((3,)), sem((3,)), sem, sem, sem((3,)), sem((5,)),
             ],
             compiler_params=pltpu.CompilerParams(collective_id=0, has_side_effects=True,
-                                                 vmem_limit_bytes=60 << 20),
+                                                 vmem_limit_bytes=63 << 20),
             name='fock',
         )(bt, ct)
 

time: 73.6 us -> 71.1 us (0.966)
  Pallas kernels: 72.8 us -> 70.3 us
    pallas_call x1, Pallas kernels: 72.8 us -> 70.3 us  [local_fock(): pl.pallas_call(kernel, out_shape=pltpu.VMEM((ROWS, HALF), f32), in_specs=...]
where the time goes in v3:
time: 71.1 us; the launch traced here: 71 us
  Pallas kernels  70.3 us (99%)
    pallas_call x1, Pallas kernels, local_fock(): pl.pallas_call(kernel, out_shape=pltpu.VMEM((ROWS, HALF), f32), in_specs=...  70.3 us

profile of v3, /device:TPU:0, one launch (start us, length us, event | category | flops | bytes accessed | tf_op | source)
XLA Modules:
  0.0 71.0 jit_solution(4107040993996379265)
XLA Ops:
  0.0 70.3 %fock.1 = f32[87,174]{1,0:T(8,128)S(1)} custom-call(f32[87,348,510]{2,1,0:T(8,128)} %bitcast.2, f32[30,348]{1,0:T(8,128)} %bitcast.3), custom_call_target="tpu_custom_call" | custom-call | tf_op jit(solution)/shard_map/fock/pallas_call | solution.py:371
  70.3 0.6 copy.4

commit v4 on v3

--- a/solution.py
+++ b/solution.py
@@ -23,6 +23,10 @@
 FIRST = 2
 ICH = 3
 NCH = NOCC // ICH
+MAIN = RPAD - GRP
+TAIL = ROWS - MAIN
+DENSE = 216
+CUTS = (0, 3, 6, 9, 12, 15, 18, 21, 24, 27, 30)
 HALF = 174
 
 
@@ -56,8 +60,8 @@
     return first[:n] + ((first[n:2 * n] + second[:n]) + small)
 
 
-def kernel(bt, ct_hbm, out, ring, ct, fb, e0, tb, sb, rb, gacc, cst, cown, gown, grecv, jt, ks, kr, rsend, rrecv,
-           pf, ph, dma_sem, ct_sem, fb_sem, e_s, e_r, d2d_s, d2d_r, ici_s, ici_r, g_s, g_r, r_s, r_r, p_s, p_r):
+def kernel(bt, ct_hbm, out, ring, ct, fb, e0, tb, sb, rb, lt, rl, gacc, cst, cown, gown, grecv, jt, ks, kr, kl, rsend, rrecv,
+           pf, ph, dma_sem, ct_sem, fb_sem, e_s, e_r, d2d_s, d2d_r, ici_s, ici_r, last_s, last_r, g_s, g_r, r_s, r_r, p_s, p_r):
     y = lax.axis_index('aux')
     o = lax.axis_index('orb')
     p = o // 2
@@ -97,14 +101,14 @@
             def _():
                 copy.wait()
 
-    def first_load(m):
+    def first_load(g):
         lanes = pl.ds(pl.multiple_of(give * 128, 128), 128)
-        return pltpu.make_async_copy(bt.at[m, :, lanes], fb.at[m], fb_sem.at[m])
+        rows = pl.ds(g * GRP, GRP)
+        return pltpu.make_async_copy(bt.at[rows, :, lanes], fb.at[rows], fb_sem.at[g])
 
     ct_copy = pltpu.make_async_copy(ct_hbm, ct, ct_sem)
     ct_copy.start()
-    for m in range(FIRST * GRP):
-        first_load(m).start()
+    first_load(0).start()
     for g in range(AHEAD):
         start_group(g, g)
 
@@ -132,9 +136,14 @@
 
     def late_copy(c):
         orbs = pl.ds(c * ICH, ICH)
-        rows = pl.ds(EARLY * GRP, RPAD - EARLY * GRP)
+        rows = pl.ds(EARLY * GRP, MAIN - EARLY * GRP)
         return remote(t4.at[pl.ds(give, 2), orbs, rows], rb.at[:, orbs, rows],
                       ici_s.at[EARLY + c], ici_r.at[EARLY + c], dev(y, opp))
+
+    def last_copy(c):
+        lo, hi = (-(-TAIL * CUTS[k] // GRP) * GRP for k in (c, c + 1))
+        rows = pl.ds(lo, hi - lo)
+        return remote(lt.at[pl.ds(give, 2), rows], rl.at[:, rows], last_s.at[c], last_r.at[c], dev(y, opp))
 
     def sib_copy(g):
         rows = pl.ds(pl.multiple_of(g * GRP, GRP), GRP)
@@ -143,6 +152,23 @@
     ct_copy.wait()
     c = jnp.concatenate([ct[...], jnp.zeros((2, NBF), f32)], axis=0)
     cst[...] = jnp.concatenate(pieces(c), axis=0)
+    def t_rows(x):
+        r = None
+        for piece in pieces(x):
+            term = jnp.dot(cst[...], piece, preferred_element_type=f32)
+            r = term if r is None else r + term
+        return r[0:32] + r[32:64] + r[64:96]
+
+    for g in range(FIRST):
+        first_load(g).wait()
+        if g + 1 < FIRST:
+            first_load(g + 1).start()
+        for j in range(GRP):
+            e0[pl.ds(g * NOCC * GRP + j, NOCC, stride=GRP), :] = t_rows(fb[g * GRP + j])[:NOCC]
+        if g == 0:
+            pl.semaphore_wait(barrier, len(peers))
+        first_copy(g).start()
+
     mine = c[:, 0:ROWS]
     for b in range(1, 4):
         mine = jnp.where(o == b, c[:, b * ROWS:(b + 1) * ROWS], mine)
@@ -151,37 +177,19 @@
     jt[...] = jnp.zeros_like(jt)
     ks[...] = jnp.zeros_like(ks)
     kr[...] = jnp.zeros_like(kr)
-
-    def t_rows(x):
-        r = None
-        for piece in pieces(x):
-            term = jnp.dot(cst[...], piece, preferred_element_type=f32)
-            r = term if r is None else r + term
-        return r[0:32] + r[32:64] + r[64:96]
-
-    for g in range(FIRST):
-        for j in range(GRP):
-            first_load(g * GRP + j).wait()
-        for j in range(GRP):
-            e0[pl.ds(g * NOCC * GRP + j, NOCC, stride=GRP), :] = t_rows(fb[g * GRP + j])[:NOCC]
-        if g == 0:
-            pl.semaphore_wait(barrier, len(peers))
-        first_copy(g).start()
-
-    def t_step(g, carry):
+    kl[...] = jnp.zeros_like(kl)
+
+    def t_group(g, rows, dense):
         slot = lax.rem(g, RING)
-
-        @pl.when(g + AHEAD < NGRP)
-        def _():
-            start_group(g + AHEAD, lax.rem(g + AHEAD, RING))
+        if not dense:
+            @pl.when(g + AHEAD < NGRP)
+            def _():
+                start_group(g + AHEAD, lax.rem(g + AHEAD, RING))
         wait_group(g, slot)
         cg = pltpu.roll(cown[...], lax.rem(128 - g * GRP, 128), 1)
-        for j in range(GRP):
+        for j in range(rows):
             m = g * GRP + j
-            x = ring[slot * GRP + j]
-            t = t_rows(x)
-            if j == GRP - 1:
-                t = jnp.where(m < ROWS, t, 0.0)
+            t = t_rows(ring[slot * GRP + j])
             gacc[:, 0:NQ] += t * cg[:, j:j + 1]
             for k in range(QT):
                 hi = min(NQ, 128 * (k + 1))
@@ -189,7 +197,12 @@
                 if hi < 128 * (k + 1):
                     tt = jnp.concatenate([tt, jnp.zeros((NOCC, 128 * (k + 1) - hi), f32)], axis=1)
                 tb[k, pl.ds(m, NOCC, stride=RPAD), :] = tt
+                if dense:
+                    lt[k, pl.ds(j, NOCC, stride=TAIL), :] = tt
         sib_copy(g).start()
+
+    def t_step(g, carry):
+        t_group(g, GRP, False)
 
         @pl.when(g < FIRST)
         def _():
@@ -200,7 +213,11 @@
             early_copy(g).start()
         return carry
 
-    lax.fori_loop(0, NGRP, t_step, 0)
+    lax.fori_loop(0, NGRP - 1, t_step, 0)
+    for k in range(QT):
+        tb[k, pl.ds(ROWS, NOCC, stride=RPAD), :] = jnp.zeros((NOCC, 128), f32)
+        lt[k, DENSE - GRP:, :] = jnp.zeros((GRP, 128), f32)
+    t_group(NGRP - 1, TAIL, True)
 
     gown[...] = jnp.sum(gacc[...], axis=0, keepdims=True)
     g_copies = [remote(gown, grecv.at[k], g_s.at[k], g_r.at[k], dev(y, to))
@@ -213,6 +230,9 @@
         return carry
 
     lax.fori_loop(0, NCH, late_start, 0)
+
+    for c in range(len(CUTS) - 1):
+        last_copy(c).start()
 
     def sib_wait(g, carry):
         sib_copy(g).wait_recv()
@@ -296,49 +316,94 @@
         early_rest(g).wait_recv()
     lax.fori_loop(FIRST, EARLY, early_wait, 0)
 
+    def k_cross(i, moved):
+        _, stack = both([t4[keep + k, i] for k in range(2)], [sb[keep + k, i] for k in range(2)])
+        return full_nt(jnp.concatenate(moved, axis=1), stack)
+
     def r_step(c, carry):
         late_copy(c).wait_recv()
         for di in range(ICH):
             i = c * ICH + di
-            _, stack = both([t4[keep + k, i] for k in range(2)], [sb[keep + k, i] for k in range(2)])
-            moved = jnp.concatenate([rb[k, i] for k in range(2)], axis=1)
-            kr[:, 0:128 + RPAD] += full_nt(moved, stack)
+            kr[:, 0:128 + RPAD] += k_cross(i, [rb[k, i, 0:MAIN] for k in range(2)])
         return carry
 
     lax.fori_loop(0, NCH, r_step, 0)
 
-    p_full0 = remote(kr, pf.at[0], p_s.at[0], p_r.at[0], dev(y, opp))
-    p_full1 = remote(kr, pf.at[1], p_s.at[0], p_r.at[1], dev(yo, opp))
-    p_own = remote(kr.at[:, pl.ds(0, 128)], ph.at[0], p_s.at[1], p_r.at[2], dev(yo, o))
-    p_sib0 = remote(kr.at[:, pl.ds(128, 128)], ph.at[1], p_s.at[2], p_r.at[3], dev(y, sib))
-    p_sib1 = remote(kr.at[:, pl.ds(128, 128)], ph.at[2], p_s.at[2], p_r.at[4], dev(yo, sib))
+    def sends(src, lo, n, base):
+        rows = pl.ds(lo, n)
+        left, right = pl.ds(0, 128), pl.ds(128, 128)
+        ss = 3 * (base // 5)
+        return (remote(src, pf.at[0, rows], p_s.at[ss], p_r.at[base], dev(y, opp)),
+                remote(src, pf.at[1, rows], p_s.at[ss], p_r.at[base + 1], dev(yo, opp)),
+                remote(src.at[:, left], ph.at[0, rows], p_s.at[ss + 1], p_r.at[base + 2], dev(yo, o)),
+                remote(src.at[:, right], ph.at[1, rows], p_s.at[ss + 2], p_r.at[base + 3], dev(y, sib)),
+                remote(src.at[:, right], ph.at[2, rows], p_s.at[ss + 2], p_r.at[base + 4], dev(yo, sib)))
+
+    main = sends(kr, 0, MAIN, 0)
+    last = sends(kl, MAIN, GRP, 5)
 
     @pl.when(y == p)
     def _():
-        for copy in (p_full0, p_sib1, p_own):
-            copy.start()
+        for k in (0, 4, 2):
+            main[k].start()
+
+    @pl.when(y != p)
+    def _():
+        main[1].start()
+        main[3].start()
+
+    def last_step(n, carry):
+        for c in range(len(CUTS) - 1):
+            @pl.when(n == CUTS[c] // ICH)
+            def _():
+                last_copy(c).wait_recv()
+        gap = jnp.zeros((GRP - TAIL, 128), f32)
+        acc = kl[:, 0:128 + RPAD]
+        for di in range(ICH):
+            i = n * ICH + di
+            acc += k_cross(i, [jnp.concatenate([rl[k, pl.ds(TAIL * i, TAIL), :], gap], axis=0) for k in range(2)])
+        kl[:, 0:128 + RPAD] = acc
+        return carry
+
+    lax.fori_loop(0, NCH, last_step, 0)
+
+    @pl.when(y == p)
+    def _():
+        for k in (0, 4, 2):
+            last[k].start()
         r_copy.wait()
         out[...] = (ks[:, 0:HALF] + rrecv[:, 0:HALF])[0:ROWS]
-        for copy in (p_full0, p_sib1, p_own):
-            copy.wait_send()
+        for k in (0, 4, 2):
+            main[k].wait_send()
+            last[k].wait_send()
 
     @pl.when(y != p)
     def _():
-        p_full1.start()
-        p_sib0.start()
+        last[1].start()
+        last[3].start()
         r_copy.wait()
-        for copy in (p_sib0, p_own, p_sib1):
-            copy.wait_recv()
-        col_opp = jnp.transpose(jnp.concatenate([kr[:, 0:128] + ph[0], jnp.zeros((40, 128), f32)], axis=0))[0:RPAD]
-        col_sib = jnp.transpose(jnp.concatenate([ph[1] + ph[2], jnp.zeros((40, 128), f32)], axis=0))[0:RPAD]
-        for copy in (p_full0, p_full1):
-            copy.wait_recv()
+
+        def turn(x):
+            return jnp.transpose(jnp.concatenate([x, jnp.zeros((40, 128), f32)], axis=0))[0:RPAD]
+
+        for k in (3, 2, 4):
+            main[k].wait_recv()
+        for k in (0, 1):
+            main[k].wait_recv()
+        for k in (3, 2, 4):
+            last[k].wait_recv()
+        mine_opp = jnp.concatenate([kr[:, 0:128], kl[:, 0:128]], axis=0)
+        col_opp = turn(mine_opp + ph[0])
+        col_sib = turn(ph[1] + ph[2])
+        for k in (0, 1):
+            last[k].wait_recv()
         block_a = (pf[0, :, 0:128] + pf[1, :, 0:128]) + col_opp
         block_b = (pf[0, :, 128:256] + pf[1, :, 128:256]) + col_sib
         res = (ks[:, 0:HALF] + rrecv[:, 0:HALF]) - columns(block_a, block_b)
         out[...] = res[0:ROWS]
-        p_full1.wait_send()
-        p_sib0.wait_send()
+        for k in (1, 3):
+            main[k].wait_send()
+            last[k].wait_send()
 
     def sends_done(g, carry):
         sib_copy(g).wait_send()
@@ -360,6 +425,9 @@
         return carry
 
     lax.fori_loop(0, NCH, late_done, 0)
+
+    for c in range(len(CUTS) - 1):
+        last_copy(c).wait_send()
 
 
 def solution(mesh):
@@ -380,7 +448,9 @@
                 pltpu.VMEM((FIRST * NOCC * GRP, 128), f32),
                 pltpu.VMEM((QT, NOCC * RPAD, 128), f32),
                 pltpu.VMEM((QT, NOCC, RPAD, 128), f32),
-                pltpu.VMEM((2, NOCC, RPAD, 128), f32),
+                pltpu.VMEM((2, NOCC, MAIN, 128), f32),
+                pltpu.VMEM((QT, DENSE, 128), f32),
+                pltpu.VMEM((2, DENSE, 128), f32),
                 pltpu.VMEM((32, 512), f32),
                 pltpu.VMEM((96, NBF), bf16),
                 pltpu.VMEM((32, 128), f32),
@@ -388,13 +458,15 @@
                 pltpu.VMEM((3, 1, 512), f32),
                 pltpu.VMEM((NBF, 128), f32),
                 pltpu.VMEM((RPAD, 256), f32),
-                pltpu.VMEM((RPAD, 256), f32),
+                pltpu.VMEM((MAIN, 256), f32),
+                pltpu.VMEM((GRP, 256), f32),
                 pltpu.VMEM((RPAD, 256), f32),
                 pltpu.VMEM((RPAD, 256), f32),
                 pltpu.VMEM((2, RPAD, 256), f32),
                 pltpu.VMEM((3, RPAD, 128), f32),
-                sem((RING * GRP,)), sem, sem((FIRST * GRP,)), sem((FIRST,)), sem((FIRST,)), sem((NGRP,)), sem((NGRP,)), sem((EARLY + NCH,)), sem((EARLY + NCH,)),
-                sem((3,)), sem((3,)), sem, sem, sem((3,)), sem((5,)),
+                sem((RING * GRP,)), sem, sem((FIRST,)), sem((FIRST,)), sem((FIRST,)), sem((NGRP,)), sem((NGRP,)), sem((EARLY + NCH,)), sem((EARLY + NCH,)),
+                sem((len(CUTS) - 1,)), sem((len(CUTS) - 1,)),
+                sem((3,)), sem((3,)), sem, sem, sem((6,)), sem((10,)),
             ],
             compiler_params=pltpu.CompilerParams(collective_id=0, has_side_effects=True,
                                                  vmem_limit_bytes=63 << 20),

time: 71.1 us -> 68.3 us (0.961)
  Pallas kernels: 70.3 us -> 67.5 us
    pallas_call x1, Pallas kernels: 70.3 us -> 67.5 us  [local_fock(): pl.pallas_call(kernel, out_shape=pltpu.VMEM((ROWS, HALF), f32), in_specs=...]
where the time goes in v4:
time: 68.3 us; the launch traced here: 68.2 us
  Pallas kernels  67.5 us (99%)
    pallas_call x1, Pallas kernels, local_fock(): pl.pallas_call(kernel, out_shape=pltpu.VMEM((ROWS, HALF), f32), in_specs=...  67.5 us

profile of v4, /device:TPU:0, one launch (start us, length us, event | category | flops | bytes accessed | tf_op | source)
XLA Modules:
  0.0 68.2 jit_solution(8044525095039735108)
XLA Ops:
  0.0 67.5 %fock.1 = f32[87,174]{1,0:T(8,128)S(1)} custom-call(f32[87,348,510]{2,1,0:T(8,128)} %bitcast.2, f32[30,348]{1,0:T(8,128)} %bitcast.3), custom_call_target="tpu_custom_call" | custom-call | tf_op jit(solution)/shard_map/fock/pallas_call | solution.py:439
  67.5 0.6 copy.4

commit v5 on v4

--- a/solution.py
+++ b/solution.py
@@ -23,6 +23,7 @@
 FIRST = 2
 ICH = 3
 NCH = NOCC // ICH
+LATE = 6
 MAIN = RPAD - GRP
 TAIL = ROWS - MAIN
 DENSE = 216
@@ -61,7 +62,7 @@
 
 
 def kernel(bt, ct_hbm, out, ring, ct, fb, e0, tb, sb, rb, lt, rl, gacc, cst, cown, gown, grecv, jt, ks, kr, kl, rsend, rrecv,
-           pf, ph, dma_sem, ct_sem, fb_sem, e_s, e_r, d2d_s, d2d_r, ici_s, ici_r, last_s, last_r, g_s, g_r, r_s, r_r, p_s, p_r):
+           pf, ph, dma_sem, ct_sem, fb_sem, d2d_s, d2d_r, ici_s, early_r, late_r, last_r, g_s, g_r, r_s, r_r, p_s, p_r):
     y = lax.axis_index('aux')
     o = lax.axis_index('orb')
     p = o // 2
@@ -80,37 +81,23 @@
         return pltpu.make_async_remote_copy(src_ref=src, dst_ref=dst, send_sem=ssem, recv_sem=rsem,
                                             device_id=to, device_id_type=pl.DeviceIdType.MESH)
 
-    def load(g, slot, j):
-        m = g * GRP + j
-        slot = slot * GRP + j
-        return m, pltpu.make_async_copy(bt.at[m], ring.at[slot], dma_sem.at[slot])
-
-    def start_group(g, slot):
-        for j in range(GRP):
-            m, copy = load(g, slot, j)
-
-            @pl.when(m < ROWS)
-            def _():
-                copy.start(priority=1)
-
-    def wait_group(g, slot):
-        for j in range(GRP):
-            m, copy = load(g, slot, j)
-
-            @pl.when(m < ROWS)
-            def _():
-                copy.wait()
+    def load(g, slot):
+        return pltpu.make_async_copy(bt.at[pl.ds(g * GRP, GRP)], ring.at[pl.ds(slot * GRP, GRP)], dma_sem.at[slot])
+
+    def tail_load():
+        slot = (NGRP - 1) % RING
+        return pltpu.make_async_copy(bt.at[pl.ds(MAIN, TAIL)], ring.at[pl.ds(slot * GRP, TAIL)], dma_sem.at[slot])
 
     def first_load(g):
         lanes = pl.ds(pl.multiple_of(give * 128, 128), 128)
         rows = pl.ds(g * GRP, GRP)
-        return pltpu.make_async_copy(bt.at[rows, :, lanes], fb.at[rows], fb_sem.at[g])
+        return pltpu.make_async_copy(bt.at[rows, :, lanes], fb.at[rows], fb_sem)
 
     ct_copy = pltpu.make_async_copy(ct_hbm, ct, ct_sem)
     ct_copy.start()
     first_load(0).start()
     for g in range(AHEAD):
-        start_group(g, g)
+        load(g, g).start(priority=1)
 
     barrier = pltpu.get_barrier_semaphore()
     peers = [(y, sib), (y, opp), (y, opp_sib), (yo, o), (yo, sib), (yo, opp), (yo, opp_sib)]
@@ -119,35 +106,42 @@
 
     t4 = tb.reshape(QT, NOCC, RPAD, 128)
 
+    def cross(src, dst, rsem):
+        return remote(src, dst, ici_s.at[0], rsem, dev(y, opp))
+
     def early_copy(g):
         rows = pl.ds(pl.multiple_of(g * GRP, GRP), GRP)
-        return remote(t4.at[pl.ds(give, 2), :, rows], rb.at[:, :, rows], ici_s.at[g], ici_r.at[g], dev(y, opp))
+        return cross(t4.at[pl.ds(give, 2), :, rows], rb.at[:, :, rows], early_r)
 
     def early_rest(g):
         rows = pl.ds(pl.multiple_of(g * GRP, GRP), GRP)
-        return remote(t4.at[pl.ds(give + 1, 1), :, rows], rb.at[pl.ds(1, 1), :, rows], ici_s.at[g], ici_r.at[g],
-                      dev(y, opp))
+        return cross(t4.at[pl.ds(give + 1, 1), :, rows], rb.at[pl.ds(1, 1), :, rows], early_r)
 
     e4 = e0.reshape(FIRST, NOCC, GRP, 128)
 
     def first_copy(g):
-        rows = pl.ds(g * GRP, GRP)
-        return remote(e4.at[g], rb.at[0, :, rows], e_s.at[g], e_r.at[g], dev(y, opp))
+        return cross(e4.at[g], rb.at[0, :, pl.ds(g * GRP, GRP)], early_r)
 
     def late_copy(c):
-        orbs = pl.ds(c * ICH, ICH)
+        orbs = pl.ds(c * LATE, LATE)
         rows = pl.ds(EARLY * GRP, MAIN - EARLY * GRP)
-        return remote(t4.at[pl.ds(give, 2), orbs, rows], rb.at[:, orbs, rows],
-                      ici_s.at[EARLY + c], ici_r.at[EARLY + c], dev(y, opp))
+        return cross(t4.at[pl.ds(give, 2), orbs, rows], rb.at[:, orbs, rows], late_r.at[c])
 
     def last_copy(c):
         lo, hi = (-(-TAIL * CUTS[k] // GRP) * GRP for k in (c, c + 1))
         rows = pl.ds(lo, hi - lo)
-        return remote(lt.at[pl.ds(give, 2), rows], rl.at[:, rows], last_s.at[c], last_r.at[c], dev(y, opp))
+        return remote(lt.at[pl.ds(give, 2), rows], rl.at[:, rows], ici_s.at[1], last_r.at[c], dev(y, opp))
+
+    early_rows = pl.ds(0, EARLY * GRP)
+    early_all = cross(t4.at[pl.ds(give, 2), :, early_rows], rb.at[:, :, early_rows], early_r)
+    main_all = cross(t4.at[pl.ds(give, 2), :, pl.ds(0, MAIN)], rb, early_r)
+    last_all = remote(lt.at[pl.ds(give, 2)], rl, ici_s.at[1], last_r.at[0], dev(y, opp))
+    sib_all = remote(t4, sb, d2d_s, d2d_r, dev(y, sib))
+    g_all = remote(grecv, grecv, g_s, g_r, dev(y, sib))
 
     def sib_copy(g):
         rows = pl.ds(pl.multiple_of(g * GRP, GRP), GRP)
-        return remote(t4.at[:, :, rows], sb.at[:, :, rows], d2d_s.at[g], d2d_r.at[g], dev(y, sib))
+        return remote(t4.at[:, :, rows], sb.at[:, :, rows], d2d_s, d2d_r, dev(y, sib))
 
     ct_copy.wait()
     c = jnp.concatenate([ct[...], jnp.zeros((2, NBF), f32)], axis=0)
@@ -181,11 +175,17 @@
 
     def t_group(g, rows, dense):
         slot = lax.rem(g, RING)
-        if not dense:
-            @pl.when(g + AHEAD < NGRP)
+        if dense:
+            tail_load().wait()
+        else:
+            @pl.when(g + AHEAD < NGRP - 1)
             def _():
-                start_group(g + AHEAD, lax.rem(g + AHEAD, RING))
-        wait_group(g, slot)
+                load(g + AHEAD, lax.rem(g + AHEAD, RING)).start(priority=1)
+
+            @pl.when(g + AHEAD == NGRP - 1)
+            def _():
+                tail_load().start(priority=1)
+            load(g, slot).wait()
         cg = pltpu.roll(cown[...], lax.rem(128 - g * GRP, 128), 1)
         for j in range(rows):
             m = g * GRP + j
@@ -220,7 +220,7 @@
     t_group(NGRP - 1, TAIL, True)
 
     gown[...] = jnp.sum(gacc[...], axis=0, keepdims=True)
-    g_copies = [remote(gown, grecv.at[k], g_s.at[k], g_r.at[k], dev(y, to))
+    g_copies = [remote(gown, grecv.at[k], g_s, g_r, dev(y, to))
                 for k, to in enumerate((sib, opp, opp_sib))]
     for copy in g_copies:
         copy.start()
@@ -229,16 +229,12 @@
         late_copy(c).start()
         return carry
 
-    lax.fori_loop(0, NCH, late_start, 0)
+    lax.fori_loop(0, NOCC // LATE, late_start, 0)
 
     for c in range(len(CUTS) - 1):
         last_copy(c).start()
 
-    def sib_wait(g, carry):
-        sib_copy(g).wait_recv()
-        return carry
-
-    lax.fori_loop(0, NGRP, sib_wait, 0)
+    sib_all.wait_recv()
 
     def both(tiles_own, tiles_sib):
         own = jnp.concatenate(tiles_own, axis=1)
@@ -258,8 +254,7 @@
     ahead = NOCC - 2 * NGRP
     lax.fori_loop(0, ahead, self_step, 0)
 
-    for copy in g_copies:
-        copy.wait()
+    g_all.wait()
     gam = gown[...] + grecv[0] + grecv[1] + grecv[2]
     gown[...] = gam
     lane = lax.broadcasted_iota(jnp.int32, (NBF, 128), 1)
@@ -270,11 +265,11 @@
 
         @pl.when((n >= 1) & (n <= AGAIN))
         def _():
-            start_group(n - 1, lax.rem(n - 1 + AGAIN, RING))
+            load(n - 1, lax.rem(n - 1 + AGAIN, RING)).start(priority=1)
 
         @pl.when(n >= RING)
         def _():
-            wait_group(g, slot)
+            load(g, slot).wait()
         gv = gown[:, 0:NQ]
         acc = jt[...]
         for j in range(GRP):
@@ -307,21 +302,16 @@
     r_copy = remote(rsend, rrecv, r_s, r_r, dev(yo, o))
     r_copy.start()
 
-    def early_wait(g, carry):
-        early_copy(g).wait_recv()
-        return carry
-
-    for g in range(FIRST):
-        first_copy(g).wait_recv()
-        early_rest(g).wait_recv()
-    lax.fori_loop(FIRST, EARLY, early_wait, 0)
+    early_all.wait_recv()
 
     def k_cross(i, moved):
         _, stack = both([t4[keep + k, i] for k in range(2)], [sb[keep + k, i] for k in range(2)])
         return full_nt(jnp.concatenate(moved, axis=1), stack)
 
     def r_step(c, carry):
-        late_copy(c).wait_recv()
+        @pl.when(lax.rem(c, LATE // ICH) == 0)
+        def _():
+            late_copy(c // (LATE // ICH)).wait_recv()
         for di in range(ICH):
             i = c * ICH + di
             kr[:, 0:128 + RPAD] += k_cross(i, [rb[k, i, 0:MAIN] for k in range(2)])
@@ -332,15 +322,19 @@
     def sends(src, lo, n, base):
         rows = pl.ds(lo, n)
         left, right = pl.ds(0, 128), pl.ds(128, 128)
-        ss = 3 * (base // 5)
-        return (remote(src, pf.at[0, rows], p_s.at[ss], p_r.at[base], dev(y, opp)),
-                remote(src, pf.at[1, rows], p_s.at[ss], p_r.at[base + 1], dev(yo, opp)),
-                remote(src.at[:, left], ph.at[0, rows], p_s.at[ss + 1], p_r.at[base + 2], dev(yo, o)),
-                remote(src.at[:, right], ph.at[1, rows], p_s.at[ss + 2], p_r.at[base + 3], dev(y, sib)),
-                remote(src.at[:, right], ph.at[2, rows], p_s.at[ss + 2], p_r.at[base + 4], dev(yo, sib)))
+        full_s, half_s = p_s.at[base], p_s.at[base + 1]
+        full_r, half_r = p_r.at[base], p_r.at[base + 1]
+        return (remote(src, pf.at[0, rows], full_s, full_r, dev(y, opp)),
+                remote(src, pf.at[1, rows], full_s, full_r, dev(yo, opp)),
+                remote(src.at[:, left], ph.at[0, rows], half_s, half_r, dev(yo, o)),
+                remote(src.at[:, right], ph.at[1, rows], half_s, half_r, dev(y, sib)),
+                remote(src.at[:, right], ph.at[2, rows], half_s, half_r, dev(yo, sib)),
+                remote(pf.at[:, rows], pf.at[:, rows], full_s, full_r, dev(y, opp)),
+                remote(ph.at[:, rows], ph.at[:, rows], half_s, half_r, dev(y, sib)),
+                remote(ph.at[pl.ds(0, 2), rows], ph.at[pl.ds(0, 2), rows], half_s, half_r, dev(y, sib)))
 
     main = sends(kr, 0, MAIN, 0)
-    last = sends(kl, MAIN, GRP, 5)
+    last = sends(kl, MAIN, GRP, 2)
 
     @pl.when(y == p)
     def _():
@@ -351,6 +345,9 @@
     def _():
         main[1].start()
         main[3].start()
+
+    sib_all.wait_send()
+    main_all.wait_send()
 
     def last_step(n, carry):
         for c in range(len(CUTS) - 1):
@@ -367,67 +364,44 @@
 
     lax.fori_loop(0, NCH, last_step, 0)
 
+    def sent():
+        last_all.wait_send()
+
     @pl.when(y == p)
     def _():
         for k in (0, 4, 2):
             last[k].start()
+        sent()
         r_copy.wait()
         out[...] = (ks[:, 0:HALF] + rrecv[:, 0:HALF])[0:ROWS]
-        for k in (0, 4, 2):
-            main[k].wait_send()
-            last[k].wait_send()
+        for group in (main, last):
+            group[0].wait_send()
+            group[7].wait_send()
 
     @pl.when(y != p)
     def _():
         last[1].start()
         last[3].start()
+        sent()
         r_copy.wait()
 
         def turn(x):
             return jnp.transpose(jnp.concatenate([x, jnp.zeros((40, 128), f32)], axis=0))[0:RPAD]
 
-        for k in (3, 2, 4):
-            main[k].wait_recv()
-        for k in (0, 1):
-            main[k].wait_recv()
-        for k in (3, 2, 4):
-            last[k].wait_recv()
+        main[6].wait_recv()
+        main[5].wait_recv()
+        last[6].wait_recv()
         mine_opp = jnp.concatenate([kr[:, 0:128], kl[:, 0:128]], axis=0)
         col_opp = turn(mine_opp + ph[0])
         col_sib = turn(ph[1] + ph[2])
-        for k in (0, 1):
-            last[k].wait_recv()
+        last[5].wait_recv()
         block_a = (pf[0, :, 0:128] + pf[1, :, 0:128]) + col_opp
         block_b = (pf[0, :, 128:256] + pf[1, :, 128:256]) + col_sib
         res = (ks[:, 0:HALF] + rrecv[:, 0:HALF]) - columns(block_a, block_b)
         out[...] = res[0:ROWS]
-        for k in (1, 3):
-            main[k].wait_send()
-            last[k].wait_send()
-
-    def sends_done(g, carry):
-        sib_copy(g).wait_send()
-        return carry
-
-    lax.fori_loop(0, NGRP, sends_done, 0)
-
-    def early_done(g, carry):
-        early_copy(g).wait_send()
-        return carry
-
-    for g in range(FIRST):
-        first_copy(g).wait_send()
-        early_rest(g).wait_send()
-    lax.fori_loop(FIRST, EARLY, early_done, 0)
-
-    def late_done(c, carry):
-        late_copy(c).wait_send()
-        return carry
-
-    lax.fori_loop(0, NCH, late_done, 0)
-
-    for c in range(len(CUTS) - 1):
-        last_copy(c).wait_send()
+        for group in (main, last):
+            group[1].wait_send()
+            group[3].wait_send()
 
 
 def solution(mesh):
@@ -464,9 +438,8 @@
                 pltpu.VMEM((RPAD, 256), f32),
                 pltpu.VMEM((2, RPAD, 256), f32),
                 pltpu.VMEM((3, RPAD, 128), f32),
-                sem((RING * GRP,)), sem, sem((FIRST,)), sem((FIRST,)), sem((FIRST,)), sem((NGRP,)), sem((NGRP,)), sem((EARLY + NCH,)), sem((EARLY + NCH,)),
-                sem((len(CUTS) - 1,)), sem((len(CUTS) - 1,)),
-                sem((3,)), sem((3,)), sem, sem, sem((6,)), sem((10,)),
+                sem((RING,)), sem, sem, sem, sem, sem((2,)), sem, sem((NOCC // LATE,)), sem((len(CUTS) - 1,)),
+                sem, sem, sem, sem, sem((4,)), sem((4,)),
             ],
             compiler_params=pltpu.CompilerParams(collective_id=0, has_side_effects=True,
                                                  vmem_limit_bytes=63 << 20),

time: 68.3 us -> 67.1 us (0.982)
  Pallas kernels: 67.5 us -> 66.4 us
    pallas_call x1, Pallas kernels: 67.5 us -> 66.4 us  [local_fock(): pl.pallas_call(kernel, out_shape=pltpu.VMEM((ROWS, HALF), f32), in_specs=...]
where the time goes in v5:
time: 67.1 us; the launch traced here: 67 us
  Pallas kernels  66.4 us (99%)
    pallas_call x1, Pallas kernels, local_fock(): pl.pallas_call(kernel, out_shape=pltpu.VMEM((ROWS, HALF), f32), in_specs=...  66.4 us

profile of v5, /device:TPU:0, one launch (start us, length us, event | category | flops | bytes accessed | tf_op | source)
XLA Modules:
  0.0 67.0 jit_solution(12226833962605032632)
XLA Ops:
  0.0 66.4 %fock.1 = f32[87,174]{1,0:T(8,128)S(1)} custom-call(f32[87,348,510]{2,1,0:T(8,128)} %bitcast.2, f32[30,348]{1,0:T(8,128)} %bitcast.3), custom_call_target="tpu_custom_call" | custom-call | tf_op jit(solution)/shard_map/fock/pallas_call | solution.py:413
  66.4 0.6 copy.4

commit v6 on v5

--- a/solution.py
+++ b/solution.py
@@ -27,7 +27,9 @@
 MAIN = RPAD - GRP
 TAIL = ROWS - MAIN
 DENSE = 216
-CUTS = (0, 3, 6, 9, 12, 15, 18, 21, 24, 27, 30)
+LSTEP = 2
+CUTS = [-(-TAIL * i // GRP) * GRP for i in range(0, NOCC + 1, LSTEP)]
+SIZES = [b - a for a, b in zip(CUTS, CUTS[1:])]
 HALF = 174
 
 
@@ -82,20 +84,21 @@
                                             device_id=to, device_id_type=pl.DeviceIdType.MESH)
 
     def load(g, slot):
-        return pltpu.make_async_copy(bt.at[pl.ds(g * GRP, GRP)], ring.at[pl.ds(slot * GRP, GRP)], dma_sem.at[slot])
+        return pltpu.make_async_copy(bt.at[pl.ds(g * GRP, GRP)], ring.at[pl.ds(slot * GRP, GRP)], dma_sem.at[lax.rem(g, 4)])
 
     def tail_load():
         slot = (NGRP - 1) % RING
-        return pltpu.make_async_copy(bt.at[pl.ds(MAIN, TAIL)], ring.at[pl.ds(slot * GRP, TAIL)], dma_sem.at[slot])
-
-    def first_load(g):
+        return pltpu.make_async_copy(bt.at[pl.ds(MAIN, TAIL)], ring.at[pl.ds(slot * GRP, TAIL)], dma_sem.at[(NGRP - 1) % 4])
+
+    def first_load(g, h):
         lanes = pl.ds(pl.multiple_of(give * 128, 128), 128)
-        rows = pl.ds(g * GRP, GRP)
-        return pltpu.make_async_copy(bt.at[rows, :, lanes], fb.at[rows], fb_sem)
+        rows = pl.ds(g * GRP + h * (GRP // 2), GRP // 2)
+        return pltpu.make_async_copy(bt.at[rows, :, lanes], fb.at[rows], fb_sem.at[h])
 
     ct_copy = pltpu.make_async_copy(ct_hbm, ct, ct_sem)
     ct_copy.start()
-    first_load(0).start()
+    first_load(0, 0).start()
+    first_load(0, 1).start()
     for g in range(AHEAD):
         load(g, g).start(priority=1)
 
@@ -128,8 +131,7 @@
         return cross(t4.at[pl.ds(give, 2), orbs, rows], rb.at[:, orbs, rows], late_r.at[c])
 
     def last_copy(c):
-        lo, hi = (-(-TAIL * CUTS[k] // GRP) * GRP for k in (c, c + 1))
-        rows = pl.ds(lo, hi - lo)
+        rows = pl.ds(CUTS[c], SIZES[c])
         return remote(lt.at[pl.ds(give, 2), rows], rl.at[:, rows], ici_s.at[1], last_r.at[c], dev(y, opp))
 
     early_rows = pl.ds(0, EARLY * GRP)
@@ -154,11 +156,13 @@
         return r[0:32] + r[32:64] + r[64:96]
 
     for g in range(FIRST):
-        first_load(g).wait()
-        if g + 1 < FIRST:
-            first_load(g + 1).start()
-        for j in range(GRP):
-            e0[pl.ds(g * NOCC * GRP + j, NOCC, stride=GRP), :] = t_rows(fb[g * GRP + j])[:NOCC]
+        for h in range(2):
+            first_load(g, h).wait()
+            if g + 1 < FIRST and h == 1:
+                first_load(g + 1, 0).start()
+                first_load(g + 1, 1).start()
+            for j in range(h * GRP // 2, (h + 1) * GRP // 2):
+                e0[pl.ds(g * NOCC * GRP + j, NOCC, stride=GRP), :] = t_rows(fb[g * GRP + j])[:NOCC]
         if g == 0:
             pl.semaphore_wait(barrier, len(peers))
         first_copy(g).start()
@@ -322,7 +326,7 @@
     def sends(src, lo, n, base):
         rows = pl.ds(lo, n)
         left, right = pl.ds(0, 128), pl.ds(128, 128)
-        full_s, half_s = p_s.at[base], p_s.at[base + 1]
+        full_s, half_s = p_s.at[0], p_s.at[1]
         full_r, half_r = p_r.at[base], p_r.at[base + 1]
         return (remote(src, pf.at[0, rows], full_s, full_r, dev(y, opp)),
                 remote(src, pf.at[1, rows], full_s, full_r, dev(yo, opp)),
@@ -335,6 +339,7 @@
 
     main = sends(kr, 0, MAIN, 0)
     last = sends(kl, MAIN, GRP, 2)
+    whole = sends(rsend, 0, RPAD, 0)
 
     @pl.when(y == p)
     def _():
@@ -350,19 +355,30 @@
     main_all.wait_send()
 
     def last_step(n, carry):
-        for c in range(len(CUTS) - 1):
-            @pl.when(n == CUTS[c] // ICH)
+        for size in sorted(set(SIZES)):
+            hit = n < 0
+            for c, rows in enumerate(SIZES):
+                if rows == size:
+                    hit = hit | (n == c)
+
+            @pl.when(hit)
             def _():
-                last_copy(c).wait_recv()
+                part = pl.ds(0, size)
+                remote(lt.at[pl.ds(give, 2), part], rl.at[:, part], ici_s.at[1], last_r.at[n], dev(y, opp)).wait_recv()
         gap = jnp.zeros((GRP - TAIL, 128), f32)
-        acc = kl[:, 0:128 + RPAD]
-        for di in range(ICH):
-            i = n * ICH + di
-            acc += k_cross(i, [jnp.concatenate([rl[k, pl.ds(TAIL * i, TAIL), :], gap], axis=0) for k in range(2)])
-        kl[:, 0:128 + RPAD] = acc
-        return carry
-
-    lax.fori_loop(0, NCH, last_step, 0)
+        own, other, moved = [], [], []
+        for di in range(LSTEP):
+            i = n * LSTEP + di
+            for k in range(2):
+                own.append(t4[keep + k, i])
+                other.append(sb[keep + k, i])
+                moved.append(jnp.concatenate([rl[k, pl.ds(TAIL * i, TAIL), :], gap], axis=0))
+        moved = jnp.concatenate(moved, axis=1)
+        kl[:, 0:RPAD] += full_nt(moved, jnp.concatenate(own, axis=1))
+        kl[:, 128:128 + RPAD] += full_nt(moved, jnp.concatenate(other, axis=1))
+        return carry
+
+    lax.fori_loop(0, NOCC // LSTEP, last_step, 0)
 
     def sent():
         last_all.wait_send()
@@ -374,9 +390,8 @@
         sent()
         r_copy.wait()
         out[...] = (ks[:, 0:HALF] + rrecv[:, 0:HALF])[0:ROWS]
-        for group in (main, last):
-            group[0].wait_send()
-            group[7].wait_send()
+        whole[0].wait_send()
+        whole[7].wait_send()
 
     @pl.when(y != p)
     def _():
@@ -399,9 +414,8 @@
         block_b = (pf[0, :, 128:256] + pf[1, :, 128:256]) + col_sib
         res = (ks[:, 0:HALF] + rrecv[:, 0:HALF]) - columns(block_a, block_b)
         out[...] = res[0:ROWS]
-        for group in (main, last):
-            group[1].wait_send()
-            group[3].wait_send()
+        whole[0].wait_send()
+        whole[3].wait_send()
 
 
 def solution(mesh):
@@ -438,8 +452,8 @@
                 pltpu.VMEM((RPAD, 256), f32),
                 pltpu.VMEM((2, RPAD, 256), f32),
                 pltpu.VMEM((3, RPAD, 128), f32),
-                sem((RING,)), sem, sem, sem, sem, sem((2,)), sem, sem((NOCC // LATE,)), sem((len(CUTS) - 1,)),
-                sem, sem, sem, sem, sem((4,)), sem((4,)),
+                sem((4,)), sem, sem((2,)), sem, sem, sem((2,)), sem, sem((NOCC // LATE,)), sem((len(CUTS) - 1,)),
+                sem, sem, sem, sem, sem((2,)), sem((4,)),
             ],
             compiler_params=pltpu.CompilerParams(collective_id=0, has_side_effects=True,
                                                  vmem_limit_bytes=63 << 20),

time: 67.1 us -> 66.8 us (level)
  no operation moved by 1% of the time
where the time goes in v6:
time: 66.8 us
  Pallas kernels  66.1 us (99%)
    pallas_call x1, Pallas kernels, local_fock(): pl.pallas_call(kernel, out_shape=pltpu.VMEM((ROWS, HALF), f32), in_specs=...  66.1 us

profile of v6, /device:TPU:0, one launch (start us, length us, event | category | flops | bytes accessed | tf_op | source)
XLA Modules:
  0.0 66.8 jit_solution(7630553948680287856)
XLA Ops:
  0.0 66.1 %fock.1 = f32[87,174]{1,0:T(8,128)S(1)} custom-call(f32[87,348,510]{2,1,0:T(8,128)} %bitcast.2, f32[30,348]{1,0:T(8,128)} %bitcast.3), custom_call_target="tpu_custom_call" | custom-call | tf_op jit(solution)/shard_map/fock/pallas_call | solution.py:427
  66.1 0.6 copy.4

commit v7 on v6

--- a/solution.py
+++ b/solution.py
@@ -28,7 +28,8 @@
 TAIL = ROWS - MAIN
 DENSE = 216
 LSTEP = 2
-CUTS = [-(-TAIL * i // GRP) * GRP for i in range(0, NOCC + 1, LSTEP)]
+SENDS = (0, 4, 8, 12, 16, 18, 20, 22, 24, 26, 28, NOCC)
+CUTS = [-(-TAIL * i // GRP) * GRP for i in SENDS]
 SIZES = [b - a for a, b in zip(CUTS, CUTS[1:])]
 HALF = 174
 
@@ -353,18 +354,19 @@
 
     sib_all.wait_send()
     main_all.wait_send()
+    r_copy.wait()
+    done = ks[:, 0:HALF] + rrecv[:, 0:HALF]
+    ks[:, 0:HALF] = done
+
+    @pl.when(y == p)
+    def _():
+        out[...] = done[0:ROWS]
 
     def last_step(n, carry):
-        for size in sorted(set(SIZES)):
-            hit = n < 0
-            for c, rows in enumerate(SIZES):
-                if rows == size:
-                    hit = hit | (n == c)
-
-            @pl.when(hit)
+        for c, first in enumerate(SENDS[:-1]):
+            @pl.when(n == first // LSTEP)
             def _():
-                part = pl.ds(0, size)
-                remote(lt.at[pl.ds(give, 2), part], rl.at[:, part], ici_s.at[1], last_r.at[n], dev(y, opp)).wait_recv()
+                last_copy(c).wait_recv()
         gap = jnp.zeros((GRP - TAIL, 128), f32)
         own, other, moved = [], [], []
         for di in range(LSTEP):
@@ -388,8 +390,6 @@
         for k in (0, 4, 2):
             last[k].start()
         sent()
-        r_copy.wait()
-        out[...] = (ks[:, 0:HALF] + rrecv[:, 0:HALF])[0:ROWS]
         whole[0].wait_send()
         whole[7].wait_send()
 
@@ -398,7 +398,6 @@
         last[1].start()
         last[3].start()
         sent()
-        r_copy.wait()
 
         def turn(x):
             return jnp.transpose(jnp.concatenate([x, jnp.zeros((40, 128), f32)], axis=0))[0:RPAD]
@@ -412,7 +411,7 @@
         last[5].wait_recv()
         block_a = (pf[0, :, 0:128] + pf[1, :, 0:128]) + col_opp
         block_b = (pf[0, :, 128:256] + pf[1, :, 128:256]) + col_sib
-        res = (ks[:, 0:HALF] + rrecv[:, 0:HALF]) - columns(block_a, block_b)
+        res = ks[:, 0:HALF] - columns(block_a, block_b)
         out[...] = res[0:ROWS]
         whole[0].wait_send()
         whole[3].wait_send()

time: 66.8 us -> 66.8 us (level)
  no operation moved by 1% of the time
where the time goes in v7:
time: 66.8 us; the launch traced here: 66.7 us
  Pallas kernels  66.1 us (99%)
    pallas_call x1, Pallas kernels, local_fock(): pl.pallas_call(kernel, out_shape=pltpu.VMEM((ROWS, HALF), f32), in_specs=...  66.1 us

profile of v7, /device:TPU:0, one launch (start us, length us, event | category | flops | bytes accessed | tf_op | source)
XLA Modules:
  0.0 66.7 jit_solution(15286757788749828842)
XLA Ops:
  0.0 66.1 %fock.1 = f32[87,174]{1,0:T(8,128)S(1)} custom-call(f32[87,348,510]{2,1,0:T(8,128)} %bitcast.2, f32[30,348]{1,0:T(8,128)} %bitcast.3), custom_call_target="tpu_custom_call" | custom-call | tf_op jit(solution)/shard_map/fock/pallas_call | solution.py:426
  66.1 0.6 copy.4
